TPU v7x, 256 devices: a whole 4x4x8 slice. The times are simulated.
256 devices in a mesh: rows: 128 (over x, z, y), cols: 2 (over core).
Axes of the slice: x: 4, y: 4, z: 8, core: 2. Of those that a mesh axis runs over, the one named last changes fastest.
Arguments:
- points: float32 [8, 32768], P(None, ('cols', 'rows')), may hold values from -6 to 6
- targets: float32 [32768], P(('cols', 'rows')), may hold values from -6 to 6
- noise: float32 [64, 32768], P(None, ('cols', 'rows')), may hold values from -6 to 6
- omega: float32 [8, 2048], P(None, 'rows'), may hold values from -12 to 12
- phase: float32 [2048], P('rows'), may hold values from -3.140625 to 3.140625
- weights: float32 [2048, 64], P('rows'), may hold values from -6 to 6
Outputs:
- posterior: float32 [64, 32768], P(None, ('cols', 'rows'))
- residual: float32 [64, 32768], P(None, ('cols', 'rows'))
All inputs are finite; a program needn't handle non-finite values.
Results may differ from a plain program's by a relative error of at most 0.02.
Values may be sent and summed in bfloat16 or wider, within the bound.
A program may use at most 64 MiB of HBM per device.

v0:
```python
import functools
import math
import jax
import jax.numpy as jnp
from jax import lax
from jax.sharding import Mesh
from jax.sharding import PartitionSpec as P

ITERS = 2
ROWS = ("rows_0", "rows_1", "rows_2")
ROWS_COLS = ("rows_0", "rows_1", "rows_2", "cols")
COLS_ROWS = ("cols", "rows_0", "rows_1", "rows_2")


def turned_gather(arrays, axis, dims):
    turned = [jnp.moveaxis(a, dim, 0) for a, dim in zip(arrays, dims)]
    both = jnp.concatenate([t.reshape(len(t), -1) for t in turned], axis=1)
    whole, at, finished = (lax.all_gather(both, axis, axis=0, tiled=True), 0, [])
    for t, dim in zip(turned, dims):
        section = whole[:, at : at + t[0].size].reshape(-1, *t.shape[1:])
        finished.append(jnp.moveaxis(section, 0, dim))
        at += t[0].size
    return tuple(finished)


def over_axes(value, axes):
    return functools.reduce(lax.psum, axes, value)


def kernel_block(left, right):
    cross = lax.dot_general(
        left,
        right,
        (((0,), (0,)), ((), ())),
        precision=lax.Precision.HIGHEST,
        preferred_element_type=jnp.float32,
    )
    left_sq = jnp.sum(left * left, 0)
    right_sq = jnp.sum(right * right, 0)
    dist = left_sq[:, None] + right_sq[None, :] - 2.0 * cross
    return jnp.exp(-2.0 * dist).astype(jnp.bfloat16)


def body(points, targets, noise, omega, phase, weights):
    wide_omega, wide_phase, wide_weights = turned_gather((omega, phase, weights), ROWS, (1, 0, 0))
    features = jnp.cos(
        lax.dot_general(
            wide_omega,
            points,
            (((0,), (0,)), ((), ())),
            precision=lax.Precision.HIGHEST,
            preferred_element_type=jnp.float32,
        )
        + wide_phase[:, None]
    )
    prior = math.sqrt(2.0 / wide_weights.shape[0]) * lax.dot_general(
        wide_weights,
        features,
        (((0,), (0,)), ((), ())),
        precision=lax.Precision.HIGHEST,
        preferred_element_type=jnp.float32,
    )
    rhs = targets[None, :] - prior - 0.5 * noise
    columns = lax.all_gather(points, ROWS_COLS, axis=1, tiled=True)
    residual = rhs
    direction = rhs
    posterior = prior
    norm_now = over_axes(jnp.sum(residual * residual, 1), ROWS_COLS)
    for step in range(ITERS):
        low = direction.astype(jnp.bfloat16)
        kernel_part = jnp.dot(
            lax.all_gather(low, ROWS_COLS, axis=1, tiled=True),
            kernel_block(columns, points),
            preferred_element_type=jnp.float32,
        )
        image = kernel_part + 0.25 * direction
        curve, mixed, square = (
            over_axes(jnp.sum(direction * image, 1), ROWS_COLS),
            over_axes(jnp.sum(residual * image, 1), ROWS_COLS),
            over_axes(jnp.sum(image * image, 1), ROWS_COLS),
        )
        alpha = norm_now / curve
        norm_next = norm_now - 2.0 * alpha * mixed + alpha * alpha * square
        posterior = posterior + alpha[:, None] * kernel_part
        residual = residual - alpha[:, None] * image
        if step + 1 < ITERS:
            direction = residual + (norm_next / norm_now)[:, None] * direction
            norm_now = norm_next
    return (posterior, residual)


def solution(mesh):
    finer = Mesh(
        mesh.devices.reshape(4, 8, 4, mesh.shape["cols"]), ("rows_0", "rows_1", "rows_2", "cols")
    )
    in_specs = (
        P(None, COLS_ROWS),
        P(COLS_ROWS),
        P(None, COLS_ROWS),
        P(None, ROWS),
        P(ROWS),
        P(ROWS, None),
    )
    out_specs = (P(None, COLS_ROWS), P(None, COLS_ROWS))
    return jax.shard_map(body, mesh=finer, in_specs=in_specs, out_specs=out_specs, check_vma=False)
```

profile of v0, /device:TPU:1, one launch (start us, length us, event | category | flops | bytes accessed | tf_op | source)
XLA Modules:
  0.0 662.3 jit_solution(5400117945138848023)
XLA Ops:
  7.2 0.0 all-gather.6.cloned.1.call-start
  7.2 0.7 all-gather.6.cloned.1.call-update
  7.9 0.0 all-gather.4.cloned.1.call-start
  7.9 0.8 copy.10
  8.7 0.7 copy.11
  9.4 0.8 pad_maximum_fusion
  10.2 300.3 %all_gather.12 = f32[2048,73]{1,0:T(8,128)S(1)} all-gather(f32[16,73]{1,0:T(8,128)S(1)} %pad_maximum_fusion), channel_id=1, replica_groups=mesh['rows_0'=4,'rows_1'=8,'rows_2'=4,'cols'=2] {'rows_0','rows_1','rows..., dimensions={0}, use_global_device_ids=true | all-gather | bytes 602688 | tf_op jit(solution)/shard_map/all_gather | solution.py:18
  310.6 0.6 slice_reduce_fusion
  311.2 6.0 fusion.4
  317.2 3.6 fusion.9
  320.8 0.0 all-gather.4.cloned.1.call-update
  320.8 0.2 all-gather.8.cloned.1.call-start
  321.1 0.7 multiply_reduce_fusion.5
  321.8 0.0 all-gather.6.cloned.1.call-done
  321.8 1.5 multiply_reduce_fusion
  323.3 33.1 %fusion.3 = bf16[32768,128]{1,0:T(8,128)(2,1)} fusion(f32[8,32768]{1,0:T(8,128)} %all-gather.6.cloned.1.call-done, f32[8,128]{1,0:T(8,128)} %param.6, f32[128]{0:T(128)S(1)} %multiply_reduce_fusion.5, f32[32768]{0:T(1024)S(1)} %multiply_reduce_fusion), kind=kOutput, calls=%fused_computation.4 | convolution fusion | flops 423624704 | bytes 9572864 | tf_op jit(solution)/shard_map/dot_general | solution.py:31
  356.4 110.6 %all-gather.4.cloned.1.call-done = bf16[64,32768]{1,0:T(8,128)(2,1)} async-done(((bf16[64,128]{1,0:T(8,128)(2,1)}), bf16[64,32768]{1,0:T(8,128)(2,1)}) %all-gather.4.cloned.1.call-update) | async-done | bytes 4194320 | tf_op jit(solution)/shard_map/all_gather | solution.py:72
  467.0 6.4 multiply_reduce_fusion.3
  473.3 8.3 %all-reduce.2 = (f32[64]{0:T(128)S(1)}, f32[64]{0:T(128)S(1)}, f32[64]{0:T(128)S(1)}) all-reduce(f32[64]{0:T(128)S(1)} %get-tuple-element.3, f32[64]{0:T(128)S(1)} %get-tuple-element.4, f32[64]{0:T(128)S(1)} %get-tuple-element.2), channel_id=1, replica_groups=mesh['rows_0'=4,'rows_1'=8,'rows_2'=4,'cols'=2] {'rows_0'}, use_global_device_ids=true, to_apply=%region_13.0 | all-reduce | flops 192 | bytes 1536 | tf_op jit(solution)/shard_map/psum | solution.py:27
  481.7 13.1 %all-reduce = (f32[64]{0:T(128)S(1)}, f32[64]{0:T(128)S(1)}, f32[64]{0:T(128)S(1)}) all-reduce(f32[64]{0:T(128)S(1)} %get-tuple-element.11, f32[64]{0:T(128)S(1)} %get-tuple-element.12, f32[64]{0:T(128)S(1)} %get-tuple-element.13), channel_id=1, replica_groups=mesh['rows_0'=4,'rows_1'=8,'rows_2'=4,'cols'=2] {'rows_1'}, use_global_device_ids=true, to_apply=%region_14.0 | all-reduce | flops 192 | bytes 1536 | tf_op jit(solution)/shard_map/psum | solution.py:27
  494.8 8.4 %all-reduce.1 = (f32[64]{0:T(128)S(1)}, f32[64]{0:T(128)S(1)}, f32[64]{0:T(128)S(1)}) all-reduce(f32[64]{0:T(128)S(1)} %get-tuple-element.5, f32[64]{0:T(128)S(1)} %get-tuple-element.6, f32[64]{0:T(128)S(1)} %get-tuple-element.7), channel_id=1, replica_groups=mesh['rows_0'=4,'rows_1'=8,'rows_2'=4,'cols'=2] {'rows_2'}, use_global_device_ids=true, to_apply=%region_15.0 | all-reduce | flops 192 | bytes 1536 | tf_op jit(solution)/shard_map/psum | solution.py:27
  503.2 10.2 %all-reduce.3 = (f32[64]{0:T(128)S(1)}, f32[64]{0:T(128)S(1)}, f32[64]{0:T(128)S(1)}) all-reduce(f32[64]{0:T(128)S(1)} %get-tuple-element.8, f32[64]{0:T(128)S(1)} %get-tuple-element.9, f32[64]{0:T(128)S(1)} %get-tuple-element.10), channel_id=1, replica_groups=mesh['rows_0'=4,'rows_1'=8,'rows_2'=4,'cols'=2] {'cols'}, use_global_device_ids=true, to_apply=%region_16.0 | all-reduce | flops 192 | bytes 1536 | tf_op jit(solution)/shard_map/psum | solution.py:27
  513.4 0.7 fusion.7
  514.1 0.0 all-gather.8.cloned.1.call-update
  514.1 94.5 %all-gather.8.cloned.1.call-done = bf16[64,32768]{1,0:T(8,128)(2,1)} async-done(((bf16[64,128]{1,0:T(8,128)(2,1)}), bf16[64,32768]{1,0:T(8,128)(2,1)}) %all-gather.8.cloned.1.call-update) | async-done | bytes 4194320 | tf_op jit(solution)/shard_map/all_gather | solution.py:72
  608.7 6.3 multiply_reduce_fusion.1
  615.0 8.3 %psum.136 = f32[64]{0:T(128)S(1)} all-reduce(f32[64]{0:T(128)S(1)} %get-tuple-element.26), channel_id=1, replica_groups=mesh['rows_0'=4,'rows_1'=8,'rows_2'=4,'cols'=2] {'rows_0'}, use_global_device_ids=true, to_apply=%region_18.0 | all-reduce | flops 64 | bytes 512 | tf_op jit(solution)/shard_map/psum | solution.py:27
  623.4 13.1 %psum.137 = f32[64]{0:T(128)S(1)} all-reduce(f32[64]{0:T(128)S(1)} %psum.136), channel_id=1, replica_groups=mesh['rows_0'=4,'rows_1'=8,'rows_2'=4,'cols'=2] {'rows_1'}, use_global_device_ids=true, to_apply=%region_19.0 | all-reduce | flops 64 | bytes 512 | tf_op jit(solution)/shard_map/psum | solution.py:27
  636.5 8.4 %psum.138 = f32[64]{0:T(128)S(1)} all-reduce(f32[64]{0:T(128)S(1)} %psum.137), channel_id=1, replica_groups=mesh['rows_0'=4,'rows_1'=8,'rows_2'=4,'cols'=2] {'rows_2'}, use_global_device_ids=true, to_apply=%region_20.0 | all-reduce | flops 64 | bytes 512 | tf_op jit(solution)/shard_map/psum | solution.py:27
  644.9 10.2 %psum.139 = f32[64]{0:T(128)S(1)} all-reduce(f32[64]{0:T(128)S(1)} %psum.138), channel_id=1, replica_groups=mesh['rows_0'=4,'rows_1'=8,'rows_2'=4,'cols'=2] {'cols'}, use_global_device_ids=true, to_apply=%region_21.0 | all-reduce | flops 64 | bytes 512 | tf_op jit(solution)/shard_map/psum | solution.py:27
  655.1 0.7 multiply_subtract_fusion
  (2 shorter events, 0.0 us)
Async XLA Ops:
  7.2 314.6 %all-gather.6.cloned.1.call-start = ((), (), s32[]{:S(2)}) async-start(), calls=%async_computation.1 | async-start | bytes 1052672 | tf_op jit(solution)/shard_map/all_gather | solution.py:64
  7.9 459.1 %all-gather.4.cloned.1.call-start = ((), (), s32[]{:S(2)}) async-start(), calls=%async_computation | async-start | bytes 4210688 | tf_op jit(solution)/shard_map/all_gather | solution.py:72
  320.8 287.8 %all-gather.8.cloned.1.call-start = ((), (), s32[]{:S(2)}) async-start(), calls=%async_computation.2 | async-start | bytes 4210688 | tf_op jit(solution)/shard_map/all_gather | solution.py:72
Sparse Core Ops, SparseCore 0:
  11.7 107.1 all-gather.5
  321.0 145.9 all-gather.3
  514.2 94.3 all-gather.7
where the time goes:
time: 663 us; the launch traced here: 662 us
  blocking collectives  380 us (57%)
  waiting for transfers between devices  206 us (31%)
  matrix products  55.4 us (8%)
  between operations  13.8 us (2%)
    all_gather x1, blocking collectives, turned_gather(): lax.all_gather(both, axis, axis=0, tiled=True)  300 us
    all_gather x2, waiting for transfers between devices, body(): lax.all_gather(low, ROWS_COLS, axis=1, tiled=True)  205 us
    psum x8, blocking collectives, over_axes(): return functools.reduce(lax.psum, axes, value)  80.1 us
    dot_general x1, matrix products, kernel_block(): lax.dot_general(left, right, (((0,), (0,)), ((), ())), precision=lax.Prec...  33.1 us
  transfers between devices with their start and end apart: 3, of which 2 were waited for; matrix products, arithmetic and copies ran while one was open for 7% of the time, Pallas kernels for 0%

commit v1 on v0

--- a/solution.py
+++ b/solution.py
@@ -15,7 +15,13 @@
 def turned_gather(arrays, axis, dims):
     turned = [jnp.moveaxis(a, dim, 0) for a, dim in zip(arrays, dims)]
     both = jnp.concatenate([t.reshape(len(t), -1) for t in turned], axis=1)
-    whole, at, finished = (lax.all_gather(both, axis, axis=0, tiled=True), 0, [])
+    whole, at, finished = (
+        jnp.concatenate(
+            lax.all_to_all(jnp.stack([both] * lax.axis_size(axis)), axis, 0, 0), axis=0
+        ),
+        0,
+        [],
+    )
     for t, dim in zip(turned, dims):
         section = whole[:, at : at + t[0].size].reshape(-1, *t.shape[1:])
         finished.append(jnp.moveaxis(section, 0, dim))

time: 663 us -> 419 us (0.63)
  blocking collectives: 380 us -> 124 us
  waiting for transfers between devices: 206 us -> 219 us
    all_gather x1 -> x0, blocking collectives: 300 us -> none  [turned_gather(): lax.all_gather(both, axis, axis=0, tiled=True)]
    all_gather x1, waiting for transfers between devices: 0.01 us -> 54.5 us  [body(): columns = lax.all_gather(points, ROWS_COLS, axis=1, tiled=True)]
    all_to_all x0 -> x1, blocking collectives: none -> 43.6 us  [turned_gather(): lax.all_to_all(jnp.stack([both] * lax.axis_size(axis)), axis, 0, 0)]
    all_gather x2, waiting for transfers between devices: 205 us -> 164 us  [body(): lax.all_gather(low, ROWS_COLS, axis=1, tiled=True)]
  transfers between devices with their start and end apart: 3 -> 3, of which waited for: 2 -> 3; matrix products, arithmetic and copies ran while one was open for 7% -> 11% of each run, Pallas kernels for 0% -> 0%
where the time goes in v1:
time: 419 us; the launch traced here: 418 us
  waiting for transfers between devices  219 us (52%)
  blocking collectives  124 us (30%)
  matrix products  55.4 us (13%)
  between operations  13.8 us (3%)
    all_gather x2, waiting for transfers between devices, body(): lax.all_gather(low, ROWS_COLS, axis=1, tiled=True)  164 us
    psum x8, blocking collectives, over_axes(): return functools.reduce(lax.psum, axes, value)  80.1 us
    all_gather x1, waiting for transfers between devices, body(): columns = lax.all_gather(points, ROWS_COLS, axis=1, tiled=True)  54.5 us
    all_to_all x1, blocking collectives, turned_gather(): lax.all_to_all(jnp.stack([both] * lax.axis_size(axis)), axis, 0, 0)  43.6 us
    dot_general x1, matrix products, kernel_block(): lax.dot_general(left, right, (((0,), (0,)), ((), ())), precision=lax.Prec...  33.1 us
    dot_general x2, matrix products, body(): jnp.dot(lax.all_gather(low, ROWS_COLS, axis=1, tiled=True), kernel_block(...  12.7 us
  transfers between devices with their start and end apart: 3, of which 3 were waited for; matrix products, arithmetic and copies ran while one was open for 11% of the time, Pallas kernels for 0%

profile of v1, /device:TPU:1, one launch (start us, length us, event | category | flops | bytes accessed | tf_op | source)
XLA Modules:
  0.0 418.0 jit_solution(11057418803850128560)
XLA Ops:
  7.2 0.0 copy-start
  7.2 0.0 all-gather.6.cloned.1.call-start
  7.2 0.7 all-gather.6.cloned.1.call-update
  7.9 0.0 all-gather.4.cloned.1.call-start
  8.0 0.8 copy.13
  8.7 0.7 copy.14
  9.4 0.8 pad_maximum_fusion
  10.2 0.1 stack.2
  10.3 43.6 %all_to_all.5 = f32[128,16,73]{2,1,0:T(8,128)S(1)} all-to-all(f32[128,16,73]{2,1,0:T(8,128)S(1)} %stack.2), channel_id=1, replica_groups=mesh['rows_0'=4,'rows_1'=8,'rows_2'=4,'cols'=2] {'rows_0','rows_1','rows..., dimensions={0} | all-to-all | bytes 1196032 | tf_op jit(solution)/shard_map/all_to_all | solution.py:20
  53.9 0.6 slice_reduce_fusion
  54.5 6.0 %fusion.4 = f32[2048,128]{1,0:T(8,128)S(1)} fusion(f32[8,128]{1,0:T(8,128)} %param.6, f32[2048,73]{1,0:T(8,128)S(1)} %bitcast.12, f32[2048]{0:T(1024)S(1)} %slice_reduce_fusion), kind=kOutput, calls=%fused_computation.6 | convolution fusion | flops 25427968 | bytes 1658880 | tf_op jit(solution)/shard_map/dot_general | solution.py:53
  60.5 3.6 fusion.9
  64.1 0.0 all-gather.4.cloned.1.call-update
  64.1 0.2 all-gather.8.cloned.1.call-start
  64.4 54.5 %all-gather.6.cloned.1.call-done = f32[8,32768]{1,0:T(8,128)} async-done(((f32[8,128]{1,0:T(8,128)}), f32[8,32768]{1,0:T(8,128)}) %all-gather.6.cloned.1.call-update) | async-done | bytes 1048592 | tf_op jit(solution)/shard_map/all_gather | solution.py:70
  118.9 1.5 multiply_reduce_fusion
  120.5 33.1 %fusion.3 = bf16[32768,128]{1,0:T(8,128)(2,1)} fusion(f32[8,32768]{1,0:T(8,128)} %all-gather.6.cloned.1.call-done, f32[8,128]{1,0:T(8,128)S(1)} %copy-done, f32[128]{0:T(128)S(1)} %multiply_reduce_fusion.5, f32[32768]{0:T(1024)S(1)} %multiply_reduce_fusion), kind=kOutput, calls=%fused_computation.4 | convolution fusion | flops 423624704 | bytes 9572864 | tf_op jit(solution)/shard_map/dot_general | solution.py:37
  153.6 69.1 %all-gather.4.cloned.1.call-done = bf16[64,32768]{1,0:T(8,128)(2,1)} async-done(((bf16[64,128]{1,0:T(8,128)(2,1)}), bf16[64,32768]{1,0:T(8,128)(2,1)}) %all-gather.4.cloned.1.call-update) | async-done | bytes 4194320 | tf_op jit(solution)/shard_map/all_gather | solution.py:78
  222.7 6.4 %multiply_reduce_fusion.3 = (f32[64]{0:T(128)S(1)}, f32[64]{0:T(128)S(1)}, f32[64]{0:T(128)S(1)}, f32[64,128]{1,0:T(8,128)S(1)}) fusion(f32[64,128]{1,0:T(8,128)S(1)} %get-tuple-element.21, bf16[64,32768]{1,0:T(8,128)(2,1)} %all-gather.4.cloned.1.call-done, bf16[32768,128]{1,0:T(8,128)(2,1)} %fusion.3), kind=kOutput, calls=%fused_computation.19 | convolution fusion | flops 536936256 | bytes 12649216 | tf_op jit(solution)/shard_map/dot_general | solution.py:77
  229.0 8.3 %all-reduce.2 = (f32[64]{0:T(128)S(1)}, f32[64]{0:T(128)S(1)}, f32[64]{0:T(128)S(1)}) all-reduce(f32[64]{0:T(128)S(1)} %get-tuple-element.3, f32[64]{0:T(128)S(1)} %get-tuple-element.4, f32[64]{0:T(128)S(1)} %get-tuple-element.2), channel_id=1, replica_groups=mesh['rows_0'=4,'rows_1'=8,'rows_2'=4,'cols'=2] {'rows_0'}, use_global_device_ids=true, to_apply=%region_13.0 | all-reduce | flops 192 | bytes 1536 | tf_op jit(solution)/shard_map/psum | solution.py:33
  237.4 13.1 %all-reduce = (f32[64]{0:T(128)S(1)}, f32[64]{0:T(128)S(1)}, f32[64]{0:T(128)S(1)}) all-reduce(f32[64]{0:T(128)S(1)} %get-tuple-element.11, f32[64]{0:T(128)S(1)} %get-tuple-element.12, f32[64]{0:T(128)S(1)} %get-tuple-element.13), channel_id=1, replica_groups=mesh['rows_0'=4,'rows_1'=8,'rows_2'=4,'cols'=2] {'rows_1'}, use_global_device_ids=true, to_apply=%region_14.0 | all-reduce | flops 192 | bytes 1536 | tf_op jit(solution)/shard_map/psum | solution.py:33
  250.5 8.4 %all-reduce.1 = (f32[64]{0:T(128)S(1)}, f32[64]{0:T(128)S(1)}, f32[64]{0:T(128)S(1)}) all-reduce(f32[64]{0:T(128)S(1)} %get-tuple-element.5, f32[64]{0:T(128)S(1)} %get-tuple-element.6, f32[64]{0:T(128)S(1)} %get-tuple-element.7), channel_id=1, replica_groups=mesh['rows_0'=4,'rows_1'=8,'rows_2'=4,'cols'=2] {'rows_2'}, use_global_device_ids=true, to_apply=%region_15.0 | all-reduce | flops 192 | bytes 1536 | tf_op jit(solution)/shard_map/psum | solution.py:33
  258.9 10.2 %all-reduce.3 = (f32[64]{0:T(128)S(1)}, f32[64]{0:T(128)S(1)}, f32[64]{0:T(128)S(1)}) all-reduce(f32[64]{0:T(128)S(1)} %get-tuple-element.8, f32[64]{0:T(128)S(1)} %get-tuple-element.9, f32[64]{0:T(128)S(1)} %get-tuple-element.10), channel_id=1, replica_groups=mesh['rows_0'=4,'rows_1'=8,'rows_2'=4,'cols'=2] {'cols'}, use_global_device_ids=true, to_apply=%region_16.0 | all-reduce | flops 192 | bytes 1536 | tf_op jit(solution)/shard_map/psum | solution.py:33
  269.1 0.7 fusion.7
  269.8 0.0 all-gather.8.cloned.1.call-update
  269.8 94.5 %all-gather.8.cloned.1.call-done = bf16[64,32768]{1,0:T(8,128)(2,1)} async-done(((bf16[64,128]{1,0:T(8,128)(2,1)}), bf16[64,32768]{1,0:T(8,128)(2,1)}) %all-gather.8.cloned.1.call-update) | async-done | bytes 4194320 | tf_op jit(solution)/shard_map/all_gather | solution.py:78
  364.4 6.3 %multiply_reduce_fusion.1 = (f32[64]{0:T(128)S(1)}, f32[64,128]{1,0:T(8,128)S(1)}) fusion(f32[64,128]{1,0:T(8,128)S(1)} %get-tuple-element.21, f32[64]{0:T(128)S(1)} %get-tuple-element.17, f32[64,128]{1,0:T(8,128)S(1)} %get-tuple-element.25, f32[64]{0:T(128)S(1)} %get-tuple-element.19, bf16[64,32768]{1,0:T(8,128)(2,1)} %all-gather.8.cloned.1.call-done, ...), kind=kOutput, calls=%fused_computation.14 | convolution fusion | flops 536952768 | bytes 12681984 | tf_op jit(solution)/shard_map/dot_general | solution.py:77
  370.7 8.3 %psum.136 = f32[64]{0:T(128)S(1)} all-reduce(f32[64]{0:T(128)S(1)} %get-tuple-element.26), channel_id=1, replica_groups=mesh['rows_0'=4,'rows_1'=8,'rows_2'=4,'cols'=2] {'rows_0'}, use_global_device_ids=true, to_apply=%region_18.0 | all-reduce | flops 64 | bytes 512 | tf_op jit(solution)/shard_map/psum | solution.py:33
  379.1 13.1 %psum.137 = f32[64]{0:T(128)S(1)} all-reduce(f32[64]{0:T(128)S(1)} %psum.136), channel_id=1, replica_groups=mesh['rows_0'=4,'rows_1'=8,'rows_2'=4,'cols'=2] {'rows_1'}, use_global_device_ids=true, to_apply=%region_19.0 | all-reduce | flops 64 | bytes 512 | tf_op jit(solution)/shard_map/psum | solution.py:33
  392.2 8.4 %psum.138 = f32[64]{0:T(128)S(1)} all-reduce(f32[64]{0:T(128)S(1)} %psum.137), channel_id=1, replica_groups=mesh['rows_0'=4,'rows_1'=8,'rows_2'=4,'cols'=2] {'rows_2'}, use_global_device_ids=true, to_apply=%region_20.0 | all-reduce | flops 64 | bytes 512 | tf_op jit(solution)/shard_map/psum | solution.py:33
  400.6 10.2 %psum.139 = f32[64]{0:T(128)S(1)} all-reduce(f32[64]{0:T(128)S(1)} %psum.138), channel_id=1, replica_groups=mesh['rows_0'=4,'rows_1'=8,'rows_2'=4,'cols'=2] {'cols'}, use_global_device_ids=true, to_apply=%region_21.0 | all-reduce | flops 64 | bytes 512 | tf_op jit(solution)/shard_map/psum | solution.py:33
  410.8 0.7 multiply_subtract_fusion
  (4 shorter events, 0.0 us)
Async XLA Ops:
  7.2 57.2 %copy-start = (f32[8,128]{1,0:T(8,128)S(1)}, f32[8,128]{1,0:T(8,128)}, u32[]{:S(2)}) copy-start(f32[8,128]{1,0:T(8,128)} %param.6) | copy-start | bytes 12292
  7.2 111.8 %all-gather.6.cloned.1.call-start = ((), (), s32[]{:S(2)}) async-start(), calls=%async_computation.2 | async-start | bytes 1052672 | tf_op jit(solution)/shard_map/all_gather | solution.py:70
  7.9 214.7 %all-gather.4.cloned.1.call-start = ((), (), s32[]{:S(2)}) async-start(), calls=%async_computation.1 | async-start | bytes 4210688 | tf_op jit(solution)/shard_map/all_gather | solution.py:78
  64.1 300.2 %all-gather.8.cloned.1.call-start = ((), (), s32[]{:S(2)}) async-start(), calls=%async_computation.3 | async-start | bytes 4210688 | tf_op jit(solution)/shard_map/all_gather | solution.py:78
Sparse Core Ops, SparseCore 0:
  11.7 107.1 all-gather.5
  123.3 99.3 all-gather.3
  269.9 94.3 all-gather.7
